TPU v7x, 32 devices: a whole 2x2x4 slice. The times are simulated.
32 devices in a mesh: row: 8 (over z, core), col: 4 (over y, x).
Axes of the slice: x: 2, y: 2, z: 4, core: 2. Of those that a mesh axis runs over, the one named last changes fastest.
Arguments:
- basis: float32 [8192, 1024], P('row', 'col'), may hold values from -6 to 6
- merge_coef: float32 [1024, 4096], P('row', 'col'), may hold values from -0.1875 to 0.1875
- panels: float32 [2, 8192, 256], P(None, ('row', 'col')), may hold values from -0.0625 to 0.0625
- factors: float32 [2, 256, 256], replicated, may hold values from -1 to 1
Outputs:
- vectors: float32 [8192, 4096], P(('row', 'col'))
- wsum: float32 [2, 256], replicated
All inputs are finite; a program needn't handle non-finite values.
Results may differ from a plain program's by a relative error of at most 0.0001.
Values sent between devices are 32-bit elements; how exact they have to be, the bound alone decides.
No kernel may reach another device: no remote copies, remote signals or barrier semaphores. Data moves between devices by JAX's collectives and lax.ppermute only.
A program may use at most 128 MiB of HBM per device.

v0:
```python
import jax
import jax.numpy as jnp
from jax import lax
from jax.sharding import PartitionSpec as P

HI = lax.Precision.HIGHEST


def matmul(left, right):
    return jnp.dot(left, right, precision=HI, preferred_element_type=jnp.float32)


def to_tall(block):
    return lax.all_to_all(block, "col", split_axis=0, concat_axis=1, tiled=True)


def per_device(basis, merge_coef, panels, factors):
    coef = lax.all_gather(merge_coef, "row", axis=0, tiled=True)
    block = matmul(lax.all_gather(basis, "col", axis=1, tiled=True), coef)
    upper = jnp.triu(factors)
    local_v = lax.all_gather(panels, "col", axis=1, tiled=True)

    def reduce_terms(terms):
        return lax.psum(terms, "row")

    field = block
    first = local_v[0]
    second = local_v[1]
    proj_one = reduce_terms(matmul(first.T, field))
    field = field - matmul(first, matmul(upper[0], proj_one))
    proj_two = reduce_terms(matmul(second.T, field))
    field = field - matmul(second, matmul(upper[1], proj_two))
    row_one = jnp.sum(proj_one, axis=1)
    row_two = jnp.sum(proj_two, axis=1)
    row_one, row_two = lax.psum((row_one, row_two), "col")
    field = to_tall(field)
    scale = jnp.sqrt(jnp.float32(field.shape[1]))
    return (field, jnp.stack([row_one, row_two]) / scale)


def solution(mesh):
    placed = (P("row", "col"), P("row", "col"), P(None, ("row", "col"), None), P())
    return jax.shard_map(
        per_device,
        mesh=mesh,
        in_specs=placed,
        out_specs=(P(("row", "col"), None), P()),
        check_vma=False,
    )
```

profile of v0, /device:TPU:0, one launch (start us, length us, event | category | flops | bytes accessed | tf_op | source)
XLA Modules:
  0.0 370.3 jit_solution(15266776425502628769)
XLA Ops:
  7.2 0.0 all-gather.4.cloned.1.call-start
  7.2 0.7 all-gather.4.cloned.1.call-update
  7.9 0.0 all-gather.6.cloned.1.call-start
  7.9 0.7 all-gather.6.cloned.1.call-update
  8.6 0.0 all-gather.8.cloned.1.call-start
  8.7 0.7 all-gather.8.cloned.1.call-update
  9.4 0.0 all-reduce.4.cloned.1.call-start
  9.4 55.6 %all-gather.4.cloned.1.call-done = f32[1024,1024]{1,0:T(8,128)} async-done(((f32[1024,256]{1,0:T(8,128)}), f32[1024,1024]{1,0:T(8,128)}) %all-gather.4.cloned.1.call-update) | async-done | bytes 4194320 | tf_op jit(solution)/shard_map/all_gather | solution.py:19
  65.0 48.5 %all-gather.6.cloned.1.call-done = f32[1024,1024]{1,0:T(8,128)} async-done(((f32[128,1024]{1,0:T(8,128)}), f32[1024,1024]{1,0:T(8,128)}) %all-gather.6.cloned.1.call-update) | async-done | bytes 4194320 | tf_op jit(solution)/shard_map/all_gather | solution.py:18
  113.5 17.5 %fusion.2 = f32[1024,1024]{1,0:T(8,128)} fusion(f32[1024,1024]{1,0:T(8,128)} %all-gather.4.cloned.1.call-done, f32[1024,1024]{1,0:T(8,128)} %all-gather.6.cloned.1.call-done), kind=kOutput, calls=%fused_computation.14 | convolution fusion | flops 12884901888 | bytes 12582912 | tf_op jit(solution)/shard_map/dot_general | solution.py:10
  131.0 0.0 copy-start.4
  131.0 18.4 %all-gather.8.cloned.1.call-done = f32[2,1024,256]{2,1,0:T(8,128)} async-done(((f32[2,256,256]{2,1,0:T(8,128)}), f32[2,1024,256]{2,1,0:T(8,128)}) %all-gather.8.cloned.1.call-update) | async-done | bytes 2097168 | tf_op jit(solution)/shard_map/all_gather | solution.py:21
  149.4 0.0 copy-start.1
  149.4 10.3 %convolution_bitcast_fusion.1 = f32[256,1024]{0,1:T(8,128)} fusion(f32[1024,1024]{1,0:T(8,128)} %fusion.2, f32[2,1024,256]{2,1,0:T(8,128)} %all-gather.8.cloned.1.call-done), kind=kOutput, calls=%fused_computation.3 | convolution fusion | flops 3221225472 | bytes 6291456 | tf_op jit(solution)/shard_map/dot_general | solution.py:10
  159.7 0.0 all-reduce.4.cloned.1.call-update
  159.7 0.0 all-reduce.6.cloned.1.call-start
  159.8 0.1 iota_compare_fusion
  159.9 0.0 copy-done.4
  159.9 0.1 broadcast_select_fusion
  159.9 59.2 %all-reduce.4.cloned.1.call-done = f32[256,1024]{0,1:T(8,128)} async-done(((f32[256,1024]{0,1:T(8,128)}), f32[256,1024]{0,1:T(8,128)}) %all-reduce.4.cloned.1.call-update) | async-done | bytes 1048592 | tf_op jit(solution)/shard_map/psum | solution.py:24
  219.2 2.3 fusion.1
  221.4 0.0 copy-done.1
  221.4 5.7 %bitcast_subtract_fusion.1 = f32[1024,1024]{1,0:T(8,128)S(1)} fusion(f32[1024,1024]{1,0:T(8,128)} %fusion.2, f32[256,1024]{1,0:T(8,128)S(1)} %fusion.1, f32[2,1024,256]{2,1,0:T(8,128)S(1)} %copy-done.1), kind=kOutput, calls=%fused_computation.1 | convolution fusion | flops 3222274048 | bytes 10485760 | tf_op jit(solution)/shard_map/dot_general | solution.py:10
  227.1 0.0 copy-start
  227.1 2.0 copy-done
  229.1 7.8 %convolution_bitcast_fusion = f32[256,1024]{0,1:T(8,128)} fusion(f32[1024,1024]{1,0:T(8,128)S(1)} %bitcast_subtract_fusion.1, f32[2,1024,256]{2,1,0:T(8,128)S(1)} %copy-done.1), kind=kOutput, calls=%fused_computation.2 | convolution fusion | flops 3221225472 | bytes 6291456 | tf_op jit(solution)/shard_map/dot_general | solution.py:10
  237.0 0.0 all-reduce.6.cloned.1.call-update
  237.0 58.5 %all-reduce.6.cloned.1.call-done = f32[256,1024]{0,1:T(8,128)} async-done(((f32[256,1024]{0,1:T(8,128)}), f32[256,1024]{0,1:T(8,128)}) %all-reduce.6.cloned.1.call-update) | async-done | bytes 1048592 | tf_op jit(solution)/shard_map/psum | solution.py:24
  295.5 2.3 fusion
  297.7 6.7 %bitcast_subtract_fusion = f32[1024,1024]{1,0:T(8,128)} fusion(f32[1024,1024]{1,0:T(8,128)} %copy-done, f32[256,1024]{1,0:T(8,128)S(1)} %fusion, f32[2,1024,256]{2,1,0:T(8,128)S(1)} %copy-done.1), kind=kOutput, calls=%fused_computation | convolution fusion | flops 3222274048 | bytes 10485760 | tf_op jit(solution)/shard_map/dot_general | solution.py:10
  304.4 0.0 copy-start.2
  304.4 0.0 copy-start.3
  304.4 5.0 %all-to-all-start = ((f32[4,256,1024]{2,1,0:T(8,128)}), f32[4,256,1024]{2,1,0:T(8,128)}, u32[]{:S(2)}, u32[]{:S(2)}) async-start(f32[4,256,1024]{2,1,0:T(8,128)} %bitcast.36), calls=%async_computation | async-start | bytes 8388608 | tf_op jit(solution)/shard_map/all_to_all | solution.py:14
  309.4 0.0 copy-done.2
  309.4 0.2 reduce_sum.18
  309.6 0.0 copy-done.3
  309.6 0.2 reduce_sum.19
  309.7 48.7 %all-reduce = (f32[1,256]{1,0:T(1,128)S(1)}, f32[1,256]{1,0:T(1,128)S(1)}) all-reduce(f32[1,256]{1,0:T(1,128)S(1)} %bitcast.39, f32[1,256]{1,0:T(1,128)S(1)} %bitcast.38), channel_id=1, replica_groups=mesh['row'=8,'col'=4] {'col'}, use_global_device_ids=true, to_apply=%region_5.6 | all-reduce | flops 512 | bytes 4096 | tf_op jit(solution)/shard_map/psum | solution.py:35
  358.4 0.6 maximum_multiply_fusion
  359.0 0.0 all-to-all-done
  359.0 4.8 %copy.7 = f32[4,32,8,1024]{3,2,0,1:T(8,128)} copy(f32[4,32,8,1024]{3,2,1,0:T(8,128)} %bitcast.12) | data formatting | bytes 8388608 | tf_op jit(solution)/shard_map/all_to_all | solution.py:14
  (1 shorter events, 0.0 us)
Async XLA Ops:
  7.2 57.8 %all-gather.4.cloned.1.call-start = ((), (), s32[]{:S(2)}) async-start(), calls=%async_computation.1 | async-start | bytes 5242880 | tf_op jit(solution)/shard_map/all_gather | solution.py:19
  7.9 105.6 %all-gather.6.cloned.1.call-start = ((), (), s32[]{:S(2)}) async-start(), calls=%async_computation.2 | async-start | bytes 4718592 | tf_op jit(solution)/shard_map/all_gather | solution.py:18
  8.6 140.7 %all-gather.8.cloned.1.call-start = ((), (), s32[]{:S(2)}) async-start(), calls=%async_computation.3 | async-start | bytes 2621440 | tf_op jit(solution)/shard_map/all_gather | solution.py:21
  9.4 209.8 %all-reduce.4.cloned.1.call-start = ((), (), s32[]{:S(2)}) async-start(), calls=%async_computation.4 | async-start | bytes 2097152 | tf_op jit(solution)/shard_map/psum | solution.py:24
  131.0 28.9 %copy-start.4 = (f32[2,256,256]{2,1,0:T(8,128)S(1)}, f32[2,256,256]{2,1,0:T(8,128)}, u32[]{:S(2)}) copy-start(f32[2,256,256]{2,1,0:T(8,128)} %param.7) | copy-start | bytes 1572868
  149.4 72.1 %copy-start.1 = (f32[2,1024,256]{2,1,0:T(8,128)S(1)}, f32[2,1024,256]{2,1,0:T(8,128)}, u32[]{:S(2)}) copy-start(f32[2,1024,256]{2,1,0:T(8,128)} %all-gather.8.cloned.1.call-done) | copy-start | bytes 6291460
  159.7 135.8 %all-reduce.6.cloned.1.call-start = ((), (), s32[]{:S(2)}) async-start(), calls=%async_computation.5 | async-start | bytes 2097152 | tf_op jit(solution)/shard_map/psum | solution.py:24
  227.1 2.0 copy-start
  304.4 5.0 %copy-start.2 = (f32[256,1024]{0,1:T(8,128)S(1)}, f32[256,1024]{0,1:T(8,128)}, u32[]{:S(2)}) copy-start(f32[256,1024]{0,1:T(8,128)} %all-reduce.4.cloned.1.call-done) | copy-start | bytes 3145732
  304.4 5.1 %copy-start.3 = (f32[256,1024]{0,1:T(8,128)S(1)}, f32[256,1024]{0,1:T(8,128)}, u32[]{:S(2)}) copy-start(f32[256,1024]{0,1:T(8,128)} %all-reduce.6.cloned.1.call-done) | copy-start | bytes 3145732
  304.4 54.5 %all-to-all-start = ((f32[4,256,1024]{2,1,0:T(8,128)}), f32[4,256,1024]{2,1,0:T(8,128)}, u32[]{:S(2)}, u32[]{:S(2)}) async-start(f32[4,256,1024]{2,1,0:T(8,128)} %bitcast.36), calls=%async_computation | async-start | bytes 8388608 | tf_op jit(solution)/shard_map/all_to_all | solution.py:14
Sparse Core Ops, SparseCore 0:
  9.8 55.1 all-gather.3
  66.6 46.8 all-gather.5
  115.3 33.9 all-gather.7
  159.8 59.2 all-reduce.3
  237.1 58.2 all-reduce.5
where the time goes:
time: 371 us; the launch traced here: 370 us
  waiting for transfers between devices  242 us (65%)
  matrix products  52.5 us (14%)
  blocking collectives  48.7 us (13%)
  between operations  13.9 us (4%)
  local copies, waits for them, and re-layouts  6.81 us (2%)
  starting transfers between devices  5.16 us (1%)
    psum x2, waiting for transfers between devices, reduce_terms(): return lax.psum(terms, 'row')  118 us
    all_gather x1, waiting for transfers between devices, per_device(): block = matmul(lax.all_gather(basis, 'col', axis=1, tiled=True), coef)  55.6 us
    dot_general x7, matrix products, matmul(): jnp.dot(left, right, precision=HI, preferred_element_type=jnp.float32)  52.5 us
    psum x1, blocking collectives, per_device(): row_one, row_two = lax.psum((row_one, row_two), 'col')  48.7 us
    all_gather x1, waiting for transfers between devices, per_device(): coef = lax.all_gather(merge_coef, 'row', axis=0, tiled=True)  48.5 us
    all_gather x1, waiting for transfers between devices, per_device(): local_v = lax.all_gather(panels, 'col', axis=1, tiled=True)  18.4 us
  transfers between devices with their start and end apart: 6, of which 5 were waited for; matrix products, arithmetic and copies ran while one was open for 5% of the time, Pallas kernels for 0%

commit v1 on v0

--- a/solution.py
+++ b/solution.py
@@ -21,7 +21,7 @@
     local_v = lax.all_gather(panels, "col", axis=1, tiled=True)
 
     def reduce_terms(terms):
-        return lax.psum(terms, "row")
+        return jnp.sum(lax.all_gather(terms, "row"), axis=0)
 
     field = block
     first = local_v[0]

time: 371 us -> 441 us (1.19); the launches traced: 370 us -> 433 us
  waiting for transfers between devices: 242 us -> 275 us
  local copies, waits for them, and re-layouts: 6.81 us -> 21.8 us
  other arithmetic: 1.06 us -> 13.9 us
  starting transfers between devices: 5.16 us -> 16.8 us
  matrix products: 52.5 us -> 47 us
  blocking collectives: 48.7 us -> 43.5 us
    all_gather x0 -> x2, waiting for transfers between devices: none -> 151 us  [reduce_terms(): return jnp.sum(lax.all_gather(terms, 'row'), axis=0)]
    psum x2 -> x0, waiting for transfers between devices: 118 us -> none  [reduce_terms(): return lax.psum(terms, 'row')]
    unnamed x10 -> x12, local copies, waits for them, and re-layouts: 2.02 us -> 17 us
    all_gather x0 -> x2, starting transfers between devices: none -> 11.8 us  [reduce_terms(): return jnp.sum(lax.all_gather(terms, 'row'), axis=0)]
    dot_general x7, matrix products: 52.5 us -> 47 us  [matmul(): jnp.dot(left, right, precision=HI, preferred_element_type=jnp.float32)]
    reduce_sum x0 -> x2, other arithmetic: none -> 5.45 us  [reduce_terms(): return jnp.sum(lax.all_gather(terms, 'row'), axis=0)]
    psum x1, blocking collectives: 48.7 us -> 43.5 us  [per_device(): row_one, row_two = lax.psum((row_one, row_two), 'col')]
  transfers between devices with their start and end apart: 6 -> 6, of which waited for: 5 -> 5; matrix products, arithmetic and copies ran while one was open for 5% -> 6% of each run, Pallas kernels for 0% -> 0%
where the time goes in v1:
time: 441 us; the launch traced here: 433 us
  waiting for transfers between devices  275 us (62%)
  matrix products  47 us (11%)
  blocking collectives  43.5 us (10%)
  local copies, waits for them, and re-layouts  21.8 us (5%)
  starting transfers between devices  16.8 us (4%)
  between operations  14.3 us (3%)
  other arithmetic  13.9 us (3%)
    all_gather x2, waiting for transfers between devices, reduce_terms(): return jnp.sum(lax.all_gather(terms, 'row'), axis=0)  151 us
    all_gather x1, waiting for transfers between devices, per_device(): block = matmul(lax.all_gather(basis, 'col', axis=1, tiled=True), coef)  55.6 us
    all_gather x1, waiting for transfers between devices, per_device(): coef = lax.all_gather(merge_coef, 'row', axis=0, tiled=True)  48.5 us
    dot_general x7, matrix products, matmul(): jnp.dot(left, right, precision=HI, preferred_element_type=jnp.float32)  47 us
    psum x1, blocking collectives, per_device(): row_one, row_two = lax.psum((row_one, row_two), 'col')  43.5 us
    all_gather x1, waiting for transfers between devices, per_device(): local_v = lax.all_gather(panels, 'col', axis=1, tiled=True)  18.4 us
    unnamed x12, local copies, waits for them, and re-layouts  17 us
    all_gather x2, starting transfers between devices, reduce_terms(): return jnp.sum(lax.all_gather(terms, 'row'), axis=0)  11.8 us
  transfers between devices with their start and end apart: 6, of which 5 were waited for; matrix products, arithmetic and copies ran while one was open for 6% of the time, Pallas kernels for 0%

profile of v1, /device:TPU:0, one launch (start us, length us, event | category | flops | bytes accessed | tf_op | source)
XLA Modules:
  0.0 432.5 jit_solution(2722929039600191419)
XLA Ops:
  7.2 0.0 all-gather.8.cloned.1.call-start
  7.2 0.7 all-gather.8.cloned.1.call-update
  7.9 0.0 all-gather.10.cloned.1.call-start
  7.9 0.7 all-gather.10.cloned.1.call-update
  8.6 0.0 all-gather.12.cloned.1.call-start
  8.7 0.7 all-gather.12.cloned.1.call-update
  9.4 0.0 all-gather.14.cloned.1.call-start
  9.4 55.6 %all-gather.8.cloned.1.call-done = f32[1024,1024]{1,0:T(8,128)} async-done(((f32[1024,256]{1,0:T(8,128)}), f32[1024,1024]{1,0:T(8,128)}) %all-gather.8.cloned.1.call-update) | async-done | bytes 4194320 | tf_op jit(solution)/shard_map/all_gather | solution.py:19
  65.0 48.5 %all-gather.10.cloned.1.call-done = f32[1024,1024]{1,0:T(8,128)} async-done(((f32[128,1024]{1,0:T(8,128)}), f32[1024,1024]{1,0:T(8,128)}) %all-gather.10.cloned.1.call-update) | async-done | bytes 4194320 | tf_op jit(solution)/shard_map/all_gather | solution.py:18
  113.5 17.5 %fusion.2 = f32[1024,1024]{1,0:T(8,128)} fusion(f32[1024,1024]{1,0:T(8,128)} %all-gather.8.cloned.1.call-done, f32[1024,1024]{1,0:T(8,128)} %all-gather.10.cloned.1.call-done), kind=kOutput, calls=%fused_computation.16 | convolution fusion | flops 12884901888 | bytes 12582912 | tf_op jit(solution)/shard_map/dot_general | solution.py:10
  131.0 0.0 copy-start.4
  131.0 18.4 %all-gather.12.cloned.1.call-done = f32[2,1024,256]{2,1,0:T(8,128)} async-done(((f32[2,256,256]{2,1,0:T(8,128)}), f32[2,1024,256]{2,1,0:T(8,128)}) %all-gather.12.cloned.1.call-update) | async-done | bytes 2097168 | tf_op jit(solution)/shard_map/all_gather | solution.py:21
  149.4 10.1 %convolution_bitcast_fusion.1 = f32[256,1024]{0,1:T(8,128)} fusion(f32[1024,1024]{1,0:T(8,128)} %fusion.2, f32[2,1024,256]{2,1,0:T(8,128)} %all-gather.12.cloned.1.call-done), kind=kOutput, calls=%fused_computation.5 | convolution fusion | flops 3221225472 | bytes 6291456 | tf_op jit(solution)/shard_map/dot_general | solution.py:10
  159.5 0.0 all-gather.14.cloned.1.call-update
  159.5 11.8 %all-gather.16.cloned.1.call-start = ((), (), s32[]{:S(2)}) async-start(), calls=%async_computation.5 | async-start | bytes 9437184 | tf_op jit(solution)/shard_map/all_gather | solution.py:24
  171.3 0.1 iota_compare_fusion
  171.4 0.0 copy-done.4
  171.4 0.1 broadcast_select_fusion
  171.5 70.2 %all-gather.14.cloned.1.call-done = f32[2048,1024]{0,1:T(8,128)} async-done(((f32[256,1024]{0,1:T(8,128)}), f32[2048,1024]{0,1:T(8,128)}) %all-gather.14.cloned.1.call-update) | async-done | bytes 8388624 | tf_op jit(solution)/shard_map/all_gather | solution.py:24
  241.7 7.5 %copy.10 = f32[128,8,8,256]{3,2,1,0:T(8,128)S(1)} copy(f32[128,8,8,256]{3,1,2,0:T(8,128)} %bitcast.46) | data formatting | bytes 16777216
  249.2 0.0 copy-start.2
  249.2 0.0 copy-start.3
  249.2 2.7 bitcast_reduce_fusion.1
  251.9 1.1 fusion.1
  253.0 0.0 copy-done.2
  253.0 0.0 copy-done.3
  253.0 3.9 bitcast_subtract_fusion.1
  257.0 0.0 copy-start
  257.0 2.0 copy-done
  259.0 8.0 %convolution_bitcast_fusion = f32[256,1024]{0,1:T(8,128)} fusion(f32[1024,1024]{1,0:T(8,128)S(1)} %bitcast_subtract_fusion.1, f32[2,1024,256]{2,1,0:T(8,128)S(1)} %copy-done.3), kind=kOutput, calls=%fused_computation.4 | convolution fusion | flops 3221225472 | bytes 6291456 | tf_op jit(solution)/shard_map/dot_general | solution.py:10
  267.0 0.0 all-gather.16.cloned.1.call-update
  267.0 80.7 %all-gather.16.cloned.1.call-done = f32[2048,1024]{0,1:T(8,128)} async-done(((f32[256,1024]{0,1:T(8,128)}), f32[2048,1024]{0,1:T(8,128)}) %all-gather.16.cloned.1.call-update) | async-done | bytes 8388624 | tf_op jit(solution)/shard_map/all_gather | solution.py:24
  347.7 7.5 %copy.11 = f32[128,8,8,256]{3,2,1,0:T(8,128)S(1)} copy(f32[128,8,8,256]{3,1,2,0:T(8,128)} %bitcast.47) | data formatting | bytes 16777216
  355.2 0.0 copy-start.1
  355.2 2.7 bitcast_reduce_fusion
  357.9 1.1 fusion
  359.0 0.0 copy-done.1
  359.0 5.3 %bitcast_subtract_fusion = f32[1024,1024]{1,0:T(8,128)} fusion(f32[1024,1024]{1,0:T(8,128)S(1)} %copy-done.1, f32[256,1024]{1,0:T(8,128)S(1)} %fusion, f32[2,1024,256]{2,1,0:T(8,128)S(1)} %copy-done.3), kind=kOutput, calls=%fused_computation.2 | convolution fusion | flops 3222274048 | bytes 10485760 | tf_op jit(solution)/shard_map/dot_general | solution.py:10
  364.3 4.8 %all-to-all-start = ((f32[4,256,1024]{2,1,0:T(8,128)}), f32[4,256,1024]{2,1,0:T(8,128)}, u32[]{:S(2)}, u32[]{:S(2)}) async-start(f32[4,256,1024]{2,1,0:T(8,128)} %bitcast.48), calls=%async_computation | async-start | bytes 8388608 | tf_op jit(solution)/shard_map/all_to_all | solution.py:14
  369.1 3.8 reduce.2
  373.0 3.8 reduce.4
  376.8 43.5 %all-reduce = (f32[1,256]{1,0:T(1,128)S(1)}, f32[1,256]{1,0:T(1,128)S(1)}) all-reduce(f32[1,256]{1,0:T(1,128)S(1)} %bitcast.51, f32[1,256]{1,0:T(1,128)S(1)} %bitcast.50), channel_id=1, replica_groups=mesh['row'=8,'col'=4] {'col'}, use_global_device_ids=true, to_apply=%region_5.6 | all-reduce | flops 512 | bytes 4096 | tf_op jit(solution)/shard_map/psum | solution.py:35
  420.3 0.6 maximum_multiply_fusion
  420.8 0.0 all-to-all-done
  420.9 4.8 %copy.9 = f32[4,32,8,1024]{3,2,0,1:T(8,128)} copy(f32[4,32,8,1024]{3,2,1,0:T(8,128)} %bitcast.12) | data formatting | bytes 8388608 | tf_op jit(solution)/shard_map/all_to_all | solution.py:14
  (5 shorter events, 0.1 us)
Async XLA Ops:
  7.2 57.8 %all-gather.8.cloned.1.call-start = ((), (), s32[]{:S(2)}) async-start(), calls=%async_computation.1 | async-start | bytes 5242880 | tf_op jit(solution)/shard_map/all_gather | solution.py:19
  7.9 105.6 %all-gather.10.cloned.1.call-start = ((), (), s32[]{:S(2)}) async-start(), calls=%async_computation.2 | async-start | bytes 4718592 | tf_op jit(solution)/shard_map/all_gather | solution.py:18
  8.6 140.7 %all-gather.12.cloned.1.call-start = ((), (), s32[]{:S(2)}) async-start(), calls=%async_computation.3 | async-start | bytes 2621440 | tf_op jit(solution)/shard_map/all_gather | solution.py:21
  9.4 232.3 %all-gather.14.cloned.1.call-start = ((), (), s32[]{:S(2)}) async-start(), calls=%async_computation.4 | async-start | bytes 9437184 | tf_op jit(solution)/shard_map/all_gather | solution.py:24
  131.0 40.4 %copy-start.4 = (f32[2,256,256]{2,1,0:T(8,128)S(1)}, f32[2,256,256]{2,1,0:T(8,128)}, u32[]{:S(2)}) copy-start(f32[2,256,256]{2,1,0:T(8,128)} %param.7) | copy-start | bytes 1572868
  159.5 188.2 %all-gather.16.cloned.1.call-start = ((), (), s32[]{:S(2)}) async-start(), calls=%async_computation.5 | async-start | bytes 9437184 | tf_op jit(solution)/shard_map/all_gather | solution.py:24
  249.2 3.8 copy-start.2
  249.2 3.8 copy-start.3
  257.0 2.0 copy-start
  355.2 3.8 copy-start.1
  364.3 56.6 %all-to-all-start = ((f32[4,256,1024]{2,1,0:T(8,128)}), f32[4,256,1024]{2,1,0:T(8,128)}, u32[]{:S(2)}, u32[]{:S(2)}) async-start(f32[4,256,1024]{2,1,0:T(8,128)} %bitcast.48), calls=%async_computation | async-start | bytes 8388608 | tf_op jit(solution)/shard_map/all_to_all | solution.py:14
Sparse Core Ops, SparseCore 0:
  9.8 55.1 all-gather.7
  66.6 46.8 all-gather.9
  115.3 33.9 all-gather.11
  159.6 82.0 all-gather.13
  267.1 80.5 all-gather.15
